TPU v7x, 32 devices: a whole 2x2x4 slice. The times are simulated.
32 devices in a mesh: scan: 2 (over y), slab: 16 (over z, x, core).
Axes of the slice: x: 2, y: 2, z: 4, core: 2. Of those that a mesh axis runs over, the one named last changes fastest.
Arguments:
- image: float32 [2, 128, 256, 128], P(None, 'slab', 'scan'), parts along dimension 2, may hold values from -6 to 6
- sensitivity: bfloat16 [12, 2, 128, 128, 128], P('scan', None, 'slab'), parts along dimension 0, may hold values from -1.5 to 1.5
- kernel: float32 [256, 256, 256], P(None, 'slab'), may hold values from 0.1 to 4
Outputs:
- normal_image: float32 [2, 128, 256, 128], P(None, 'slab', 'scan'), parts along dimension 2
There are 2 independent parts, one for each index of `scan`. A program takes and returns all parts, laid end to end along the dimension named above; an argument that names none is the same for every part. Nothing has to cross between parts.
All inputs are finite; a program needn't handle non-finite values.
Results may differ from a plain program's by a relative error of at most 0.0024.
Values may be sent and summed in bfloat16 or wider, within the bound.
A program may use at most 128 MiB of HBM per device.

v0:
```python
import functools
import math

import jax
import jax.numpy as jnp
import numpy as np
from jax import lax
from jax.experimental import pallas as pl
from jax.experimental.pallas import tpu as pltpu
from jax.sharding import PartitionSpec as P

MESH = pl.DeviceIdType.MESH
smooth_weight = 0.1
F32 = jnp.float32
BF16 = jnp.bfloat16


def factor(count_out, count_in, length, sign_value):
    phases = np.outer(np.arange(count_out), np.arange(count_in)) % length
    angles = phases * (2.0 * math.pi / length)
    scale = 1.0 / math.sqrt(length)
    real, imag = np.cos(angles) * scale, sign_value * np.sin(angles) * scale
    return np.block([[real, -imag], [imag, real]]).astype(jnp.bfloat16)


def dot(a, b):
    return jnp.dot(a, b, preferred_element_type=F32)


def shifted(cells, step, axis):
    count = cells.shape[axis]
    index = lax.broadcasted_iota(jnp.int32, cells.shape, axis)
    edge = 0 if step == 1 else count - 1
    return jnp.where(index == edge, 0.0, pltpu.roll(cells, step % count, axis))


def kernel_body(
    n, image, sens, weight, fy, fzt, fx, hx, hzt, hy, out,
    sent, got, back, home, rows, halo, filt,
    other_sens, mine, other_image, other_out, total, other_total,
    send1, recv1, send2, recv2, hsend, hrecv, wsem, psend, precv, tsend, trecv,
):
    me = lax.axis_index("slab")
    coils, _, xs, ny, nz = sens.shape
    gx, gz = fx.shape[0] // 2, weight.shape[1]
    nx, gy = n * xs, fy.shape[0] // 2
    kys = gy // n
    part = kys * xs
    pair = 16 // xs
    nh = n // 2
    half, place = me // nh, lax.rem(me, nh)
    far = lax.rem(me + nh, n)
    far_half = 1 - half
    mid = coils // 2

    columns = [
        pltpu.make_async_copy(weight.at[:, pl.ds(i * 128, 128)], filt.at[i], wsem.at[i])
        for i in range(gz // 128)
    ]
    for copy in columns:
        copy.start()

    barrier = pltpu.get_barrier_semaphore()

    @pl.loop(1, n)
    def _(k):
        pl.semaphore_signal(barrier, inc=1, device_id={"slab": lax.rem(me + k, n)}, device_id_type=MESH)

    pl.semaphore_wait(barrier, n - 1)

    def halo_copy(p, side):
        plane = xs - 1 if side == 0 else 0
        to = me + 1 if side == 0 else me - 1
        return pltpu.make_async_remote_copy(
            src_ref=image.at[p, plane], dst_ref=halo.at[side, p],
            send_sem=hsend.at[side, p], recv_sem=hrecv.at[side, p],
            device_id={"slab": lax.rem(to + n, n)}, device_id_type=MESH)

    def to_far(source, target, send_sem, recv_sem):
        return pltpu.make_async_remote_copy(
            src_ref=source, dst_ref=target, send_sem=send_sem, recv_sem=recv_sem,
            device_id={"slab": far}, device_id_type=MESH)

    def maps(c):
        return to_far(sens.at[c], other_sens.at[c], psend.at[c], precv.at[c])

    image_copy = to_far(mine, other_image, tsend.at[0], trecv.at[0])
    total_copy = to_far(total, other_total, tsend.at[1], trecv.at[1])

    def block(source, target, c, to, slot, landing, send_sem, recv_sem):
        return pltpu.make_async_remote_copy(
            src_ref=source.at[c, slot], dst_ref=target.at[c, landing],
            send_sem=send_sem.at[c, slot], recv_sem=recv_sem.at[c, landing],
            device_id={"slab": to}, device_id_type=MESH)

    def over_all(source, target, c, send_sem, recv_sem, action):
        @pl.loop(1, n)
        def _(k):
            to = lax.rem(me + k, n)
            landing = to if action == "recv" else me
            act(block(source, target, c, to, to, landing, send_sem, recv_sem), action)

    def over_half(source, target, c, send_sem, recv_sem, action):
        @pl.loop(1, nh)
        def _(k):
            near = lax.rem(place + k, nh)
            for g in range(2):
                landing = near if action == "recv" else place
                act(block(source, target, c, half * nh + near, g * nh + near, g * nh + landing,
                          send_sem, recv_sem), action)

    def act(copy, action):
        if action == "start":
            copy.start()
        elif action == "recv":
            copy.wait_recv()
        else:
            copy.wait_send()

    def is_split(c):
        return lax.rem(c, mid) != 0

    def either(c, first, second):
        pl.when(is_split(c))(first)
        pl.when(jnp.logical_not(is_split(c)))(second)

    def traffic(source, target, c, send_sem, recv_sem, action):
        either(c,
               lambda: over_half(source, target, c, send_sem, recv_sem, action),
               lambda: over_all(source, target, c, send_sem, recv_sem, action))

    def start_all(source, target, c, send_sem, recv_sem):
        over_all(source, target, c, send_sem, recv_sem, "start")
        target[c, me] = source[c, me]

    def start_half(source, target, c, send_sem, recv_sem):
        over_half(source, target, c, send_sem, recv_sem, "start")
        for g in range(2):
            target[c, g * nh + place] = source[c, g * nh + place]

    def along_second(table, maps_of, cells_of):
        count = table.shape[0]

        @pl.loop(0, xs // 2)
        def _(h):
            halves = []
            for j in range(2):
                x = 2 * h + j
                cr, ci = maps_of(0, x).astype(F32), maps_of(1, x).astype(F32)
                vr, vi = cells_of(0, x).astype(F32), cells_of(1, x).astype(F32)
                halves.append(jnp.concatenate([cr * vr - ci * vi, cr * vi + ci * vr], axis=0).astype(BF16))
            lines = dot(table, jnp.concatenate(halves, axis=1))
            for j in range(2):
                rows[pl.ds(2 * h + j, count, stride=xs), :] = lines[:, j * nz:(j + 1) * nz]

    def forward_all(c):
        along_second(fy[...], lambda p, x: sens[c, p, x], lambda p, x: image[p, x])
        size = gy * xs
        for q in range(2):
            sent[c, :, q * part:(q + 1) * part, :] = (
                rows[q * size:(q + 1) * size, :].reshape(n, part, nz).astype(BF16))
        start_all(sent, got, c, send1, recv1)

    gh = gy // 2

    def forward_half(c):
        maps(c).wait_recv()
        table = jnp.concatenate(
            [fy[pl.ds(pl.multiple_of(q * gy + half * gh, gh), gh), :] for q in range(2)], axis=0)
        size = gh * xs
        for own in (True, False):
            if own:
                along_second(table, lambda p, x: sens[c, p, x], lambda p, x: image[p, x])
            else:
                along_second(table, lambda p, x: other_sens[c, p, x], lambda p, x: other_image[p, x])
            start = (half if own else far_half) * nh
            for q in range(2):
                sent[c, pl.ds(start, nh), q * part:(q + 1) * part, :] = (
                    rows[q * size:(q + 1) * size, :].reshape(nh, part, nz).astype(BF16))
        start_half(sent, got, c, send1, recv1)

    def middle(c):
        @pl.loop(0, kys // pair)
        def _(kp):
            base = pl.multiple_of(kp * 16, 16)
            cells = [got[c, :, pl.ds(q * part + base, 16), :].reshape(n * 16, nz) for q in range(2)]
            third = dot(jnp.concatenate(cells, axis=1), fzt[...]).reshape(n, pair, xs, 2 * gz)
            results = []
            for j in range(pair):
                b = third[:, j].reshape(nx, 2 * gz).astype(BF16)
                spectrum = dot(fx[...], jnp.concatenate([b[:, :gz], b[:, gz:]], axis=0))
                k = jnp.concatenate(
                    [filt[i, pl.ds(kp * pair + j, gx, stride=kys), :] for i in range(gz // 128)], axis=1)
                filtered = jnp.concatenate([spectrum[:gx] * k, spectrum[gx:] * k], axis=0).astype(BF16)
                first = dot(hx[...], filtered).astype(BF16)
                results.append(dot(jnp.concatenate([first[:nx], first[nx:]], axis=1), hzt[...]))
            for q in range(2):
                parts = [r[:, q * nz:(q + 1) * nz].reshape(n, 1, xs, nz) for r in results]
                back[c, :, pl.ds(q * part + base, 16), :] = (
                    jnp.concatenate(parts, axis=1).reshape(n, 16, nz).astype(BF16))

    def gather(table, count, maps_of, acc):
        @pl.loop(0, xs // 2)
        def _(h):
            lines = [rows[pl.ds(2 * h + j, count, stride=xs), :] for j in range(2)]
            cells = dot(table, jnp.concatenate(lines, axis=1).astype(BF16))
            for j in range(2):
                x = 2 * h + j
                re, im = cells[:ny, j * nz:(j + 1) * nz], cells[ny:, j * nz:(j + 1) * nz]
                cr, ci = maps_of(0, x).astype(F32), maps_of(1, x).astype(F32)
                acc[0, x] = acc[0, x] + cr * re + ci * im
                acc[1, x] = acc[1, x] + cr * im - ci * re

    def inverse_all(c):
        over_all(back, home, c, send2, recv2, "recv")
        size = gy * xs
        for q in range(2):
            rows[q * size:(q + 1) * size, :] = home[c, :, q * part:(q + 1) * part, :].reshape(size, nz).astype(F32)
        gather(hy[...], 2 * gy, lambda p, x: sens[c, p, x], out)

    def inverse_half(c):
        over_half(back, home, c, send2, recv2, "recv")
        table = jnp.concatenate(
            [hy[:, pl.ds(pl.multiple_of(q * gy + half * gh, gh), gh)] for q in range(2)], axis=1)
        size = gh * xs
        for own in (False, True):
            start = (half if own else far_half) * nh
            for q in range(2):
                rows[q * size:(q + 1) * size, :] = (
                    home[c, pl.ds(start, nh), q * part:(q + 1) * part, :].reshape(size, nz).astype(F32))
            if own:
                gather(table, 2 * gh, lambda p, x: sens[c, p, x], out)
            else:
                gather(table, 2 * gh, lambda p, x: other_sens[c, p, x], other_out)

    mine[...] = image[...].astype(BF16)
    maps(1).start()
    image_copy.start()
    forward_all(0)
    maps(2).start()

    @pl.when(me < n - 1)
    def _():
        for p in range(2):
            halo_copy(p, 0).start()

    @pl.when(me > 0)
    def _():
        for p in range(2):
            halo_copy(p, 1).start()

    other_out[...] = jnp.zeros_like(other_out)
    out[...] = jnp.zeros_like(out)
    image_copy.wait_recv()
    forward_half(1)
    for copy in columns:
        copy.wait()

    @pl.loop(0, coils)
    def _(c):
        @pl.when(c < mid - 1)
        def _():
            maps(c + mid + 1).start()

        @pl.when(c == 0)
        def _():
            forward_half(2)
            forward_all(mid)

        @pl.when(jnp.logical_and(c > 0, c < mid))
        def _():
            forward_half(c + mid)

        traffic(sent, got, c, send1, recv1, "recv")
        middle(c)
        either(c,
               lambda: start_half(back, home, c, send2, recv2),
               lambda: start_all(back, home, c, send2, recv2))

        @pl.when(jnp.logical_and(c >= mid, c < coils - 1))
        def _():
            inverse_half(c - mid + 1)

    @pl.loop(mid + 1, coils)
    def _(c):
        inverse_half(c)

    total[...] = other_out[...].astype(BF16)
    total_copy.start()
    inverse_all(0)

    @pl.when(me < n - 1)
    def _():
        for p in range(2):
            halo_copy(p, 0).wait_send()
            halo_copy(p, 1).wait_recv()

    @pl.when(me > 0)
    def _():
        for p in range(2):
            halo_copy(p, 1).wait_send()
            halo_copy(p, 0).wait_recv()

    for p in range(2):
        for x in range(xs):
            here = image[p, x]
            if x == 0:
                before = jnp.where(me > 0, halo[0, p], 0.0)
            else:
                before = image[p, x - 1]
            if x == xs - 1:
                after = jnp.where(me < n - 1, halo[1, p], 0.0)
            else:
                after = image[p, x + 1]
            beside = before + after
            for axis in range(2):
                beside = beside + shifted(here, 1, axis) + shifted(here, -1, axis)
            out[p, x] = out[p, x] + smooth_weight * (6.0 * here - beside)

    inverse_all(mid)
    total_copy.wait_recv()
    out[...] = out[...] + other_total[...].astype(F32)

    @pl.loop(0, coils)
    def _(c):
        traffic(sent, got, c, send1, recv1, "send")
        traffic(back, home, c, send2, recv2, "send")

    @pl.loop(1, mid)
    def _(c):
        maps(c).wait_send()
        maps(c + mid).wait_send()

    image_copy.wait_send()
    total_copy.wait_send()


def fused(n, image, sensitivity, kernel):
    coils, _, xs, ny, nz = sensitivity.shape
    gx, kys, gz = kernel.shape
    nx, gy = n * xs, n * kys
    block = (coils, n, 2 * kys * xs, nz)
    tables = (
        factor(gy, ny, gy, -1.0),
        factor(gz, nz, gz, -1.0).T,
        factor(gx, nx, gx, -1.0),
        factor(nx, gx, gx, 1.0),
        factor(nz, gz, gz, 1.0).T,
        factor(ny, gy, gy, 1.0),
    )
    vmem = pl.BlockSpec(memory_space=pltpu.VMEM)
    dma = pltpu.SemaphoreType.DMA
    return pl.pallas_call(
        functools.partial(kernel_body, n),
        out_shape=jax.ShapeDtypeStruct(image.shape, F32),
        in_specs=[vmem] * 2 + [pl.BlockSpec(memory_space=pl.ANY)] + [vmem] * 6,
        out_specs=vmem,
        scratch_shapes=[pltpu.VMEM(block, BF16)] * 4
        + [pltpu.VMEM((2 * gy * xs, nz), F32), pltpu.VMEM((2, 2, ny, nz), F32),
           pltpu.VMEM((gz // 128, gx * kys, 128), F32)]
        + [pltpu.VMEM(sensitivity.shape, BF16)]
        + [pltpu.VMEM(image.shape, BF16)] * 2 + [pltpu.VMEM(image.shape, F32)]
        + [pltpu.VMEM(image.shape, BF16)] * 2
        + [dma((coils, n))] * 4 + [dma((2, 2))] * 2 + [dma((gz // 128,))]
        + [dma((coils,))] * 2 + [dma((2,))] * 2,
        compiler_params=pltpu.CompilerParams(
            collective_id=0, has_side_effects=True, vmem_limit_bytes=62 * 2**20),
    )(image, sensitivity, kernel.reshape(gx * kys, gz), *[jnp.asarray(t) for t in tables])


def with_halo(cells, axis, dim):
    count = lax.axis_size(axis)
    head = lax.slice_in_dim(cells, 0, 1, axis=dim)
    tail = lax.slice_in_dim(cells, cells.shape[dim] - 1, cells.shape[dim], axis=dim)
    return jnp.concatenate(
        [
            lax.ppermute(tail, axis, [(i, i + 1) for i in range(count - 1)]),
            cells,
            lax.ppermute(head, axis, [(i + 1, i) for i in range(count - 1)]),
        ],
        axis=dim,
    )


def staged(n, image, sensitivity, kernel):
    coils, _, xs, ny, nz = sensitivity.shape
    gx, kys, gz = kernel.shape
    nx, gy = n * xs, n * kys

    def table(count_out, count_in, length, sign_value):
        both = factor(count_out, count_in, length, sign_value)
        return jnp.asarray(both.reshape(2, count_out, 2, count_in).transpose(0, 2, 1, 3))

    def apply(matrix, values, pattern):
        return jnp.einsum(pattern, matrix, values, preferred_element_type=F32)

    real, imag = sensitivity[:, 0].astype(F32), sensitivity[:, 1].astype(F32)
    images = jnp.stack(
        [real * image[0] - imag * image[1], real * image[1] + imag * image[0]], axis=1).astype(BF16)
    second = apply(table(gy, ny, gy, -1.0), images, "pqkj,cqajb->cpakb").astype(BF16)
    second = lax.all_to_all(second, "slab", split_axis=3, concat_axis=2, tiled=True)
    third = apply(table(gz, nz, gz, -1.0), second, "pqkj,cqabj->cpabk").astype(BF16)
    spectrum = apply(table(gx, nx, gx, -1.0), third, "pqkj,cqjab->cpkab")
    filtered = (spectrum * kernel).astype(BF16)
    first = apply(table(nx, gx, gx, 1.0), filtered, "pqkj,cqjab->cpkab").astype(BF16)
    back = apply(table(nz, gz, gz, 1.0), first, "pqkj,cqabj->cpabk").astype(BF16)
    back = lax.all_to_all(back, "slab", split_axis=2, concat_axis=3, tiled=True)
    cells = apply(table(ny, gy, gy, 1.0), back, "pqkj,cqajb->cpakb")
    summed = jnp.stack([
        jnp.sum(real * cells[:, 0] + imag * cells[:, 1], axis=0),
        jnp.sum(real * cells[:, 1] - imag * cells[:, 0], axis=0)])
    padded = with_halo(image.astype(BF16), "slab", 1).astype(image.dtype)
    beside = padded[:, 2:] + padded[:, :-2]
    wide = jnp.pad(image, ((0, 0), (0, 0), (1, 1), (1, 1)))
    beside = beside + wide[:, :, 2:, 1:-1] + wide[:, :, :-2, 1:-1]
    beside = beside + wide[:, :, 1:-1, 2:] + wide[:, :, 1:-1, :-2]
    return summed + smooth_weight * (6.0 * image - beside)


def solution(mesh):
    n = mesh.shape["slab"]

    def local(image, sensitivity, kernel):
        tiled = sensitivity.shape[2] == 8 and kernel.shape[1] % 2 == 0 and n % 2 == 0 and sensitivity.shape[0] == 6
        form = fused if tiled else staged
        return form(n, image, sensitivity, kernel)

    return jax.shard_map(
        local,
        mesh=mesh,
        in_specs=(
            P(None, "slab", "scan", None),
            P("scan", None, "slab", None, None),
            P(None, "slab", None),
        ),
        out_specs=P(None, "slab", "scan", None),
        check_vma=False,
    )
```

profile of v0, /device:TPU:27, one launch (start us, length us, event | category | flops | bytes accessed | tf_op | source)
XLA Modules:
  0.0 290.0 jit_solution(15354241705622936348)
XLA Ops:
  0.0 287.7 %shard_map.91 = f32[2,8,128,128]{3,2,1,0:T(8,128)} custom-call(f32[2,8,128,128]{3,2,1,0:T(8,128)} %image.1, bf16[6,2,8,128,128]{4,3,2,1,0:T(8,128)(2,1)} %sens.1, f32[4096,256]{1,0:T(8,128)} %bitcast.1, bf16[512,256]{1,0:T(8,128)(2,1)} %constant.4.clone.fy.fx.hzt, bf16[256,512]{1,0:T(8,128)(2,1)} %constant.5.clone.fzt.hx.hy, ...), custom_call_target="tpu_custom_call" | custom-call | tf_op jit(solution)/shard_map/pallas_call | solution.py:353
  287.7 2.3 copy.11
where the time goes:
time: 290 us
  Pallas kernels  288 us (99%)
    pallas_call x1, Pallas kernels, fused(): pl.pallas_call(functools.partial(kernel_body, n), out_shape=jax.ShapeDtyp...  288 us

commit v1 on v0

v1 whole, which is shorter than its diff:
```python
import functools
import math

import jax
import jax.numpy as jnp
import numpy as np
from jax import lax
from jax.experimental import pallas as pl
from jax.experimental.pallas import tpu as pltpu
from jax.sharding import PartitionSpec as P

MESH = pl.DeviceIdType.MESH
smooth_weight = 0.1
F32 = jnp.float32
BF16 = jnp.bfloat16


def factor(count_out, count_in, length, sign_value):
    phases = np.outer(np.arange(count_out), np.arange(count_in)) % length
    angles = phases * (2.0 * math.pi / length)
    scale = 1.0 / math.sqrt(length)
    real, imag = np.cos(angles) * scale, sign_value * np.sin(angles) * scale
    return np.block([[real, -imag], [imag, real]]).astype(jnp.bfloat16)


def dot(a, b):
    return jnp.dot(a, b, preferred_element_type=F32)


def shifted(cells, step, axis):
    count = cells.shape[axis]
    index = lax.broadcasted_iota(jnp.int32, cells.shape, axis)
    edge = 0 if step == 1 else count - 1
    return jnp.where(index == edge, 0.0, pltpu.roll(cells, step % count, axis))


PLANES = 4


def kernel_body(
    n, image, sens, weight, fy, fzt, fx, hx, hzt, hy, out,
    sent, got, home, rows, halo, filt, maps, images, mine, sums, parts, totals,
    send1, recv1, send2, recv2, hsend, hrecv, wsem, msend, mrecv, isend, irecv, tsend, trecv,
):
    me = lax.axis_index("slab")
    coils, _, xs, ny, nz = sens.shape
    gx, gz = fx.shape[0] // 2, weight.shape[1]
    nx, gy = n * xs, fy.shape[0] // 2
    kys = gy // n
    part = kys * xs
    pair = 16 // xs
    last = coils - 1
    cols = n // PLANES
    wide = gy // PLANES
    size = wide * xs
    plane, col = me // cols, lax.rem(me, cols)
    half = plane // 2
    end, mid = 3 * half, 1 + half
    other_mid, other_end = 2 - half, 3 - 3 * half
    hosted = (mid, end, other_mid, other_end)
    is_mid = plane == mid

    columns = [
        pltpu.make_async_copy(weight.at[:, pl.ds(i * 128, 128)], filt.at[i], wsem.at[i])
        for i in range(gz // 128)
    ]
    for copy in columns:
        copy.start()

    barrier = pltpu.get_barrier_semaphore()

    @pl.loop(1, n)
    def _(k):
        pl.semaphore_signal(barrier, inc=1, device_id={"slab": lax.rem(me + k, n)}, device_id_type=MESH)

    pl.semaphore_wait(barrier, n - 1)

    def remote(source, target, send_sem, recv_sem, to):
        return pltpu.make_async_remote_copy(
            src_ref=source, dst_ref=target, send_sem=send_sem, recv_sem=recv_sem,
            device_id={"slab": to}, device_id_type=MESH)

    def halo_copy(p, side):
        edge = xs - 1 if side == 0 else 0
        to = me + 1 if side == 0 else me - 1
        return remote(image.at[p, edge], halo.at[side, p], hsend.at[side, p], hrecv.at[side, p],
                      lax.rem(to + n, n))

    def map_copy(kind, c):
        source = maps.at[0, c] if kind == 2 else sens.at[c]
        to = (mid if kind == 0 else other_mid) * cols + col
        return remote(source, maps.at[kind, c], msend.at[kind, c], mrecv.at[kind, c], to)

    def image_copy(kind):
        source = images.at[0] if kind == 2 else mine
        to = (mid if kind == 0 else other_mid) * cols + col
        return remote(source, images.at[kind], isend.at[kind], irecv.at[kind], to)

    def total_copy(slot):
        landing = 1 if slot == 3 else 0
        return remote(parts.at[slot - 1], totals.at[landing], tsend.at[slot - 1], trecv.at[landing],
                      hosted[slot] * cols + col)

    def act(copy, action):
        if action == "start":
            copy.start()
        elif action == "recv":
            copy.wait_recv()
        else:
            copy.wait_send()

    def around(first, body):
        @pl.loop(first, cols)
        def _(k):
            body(lax.rem(col + k, cols))

    def sent_copy(c, slot, landing, to):
        return remote(sent.at[c, slot], got.at[c, landing], send1.at[c, slot], recv1.at[c, landing], to)

    def back_copy(c, slot, landing, to):
        return remote(got.at[c, slot], home.at[c, landing], send2.at[c, slot], recv2.at[c, landing], to)

    def all_traffic(copy_of, action):
        @pl.loop(1, n)
        def _(k):
            to = lax.rem(me + k, n)
            act(copy_of(last, to, to if action == "recv" else me, to), action)

    def own_plane_out(c, s, action):
        block = (plane if s == 0 else hosted[s]) * cols + col
        around(1, lambda near: act(
            sent_copy(c, s * cols + near, block, plane * cols + near), action))

    def end_plane_out(c, s, action):
        around(0, lambda near: act(
            sent_copy(c, (4 + s) * cols + near, hosted[s] * cols + col, end * cols + near), action))

    def keep_own(c, s):
        got[c, (plane if s == 0 else hosted[s]) * cols + col] = sent[c, s * cols + col]

    def forward_out(c, slots, action):
        for s in slots:
            own_plane_out(c, s, action)
            if s != 1:
                end_plane_out(c, s, action)

    def got_wait(c):
        @pl.when(is_mid)
        def _():
            for s in range(4):
                around(1, lambda near: sent_copy(
                    c, near, hosted[s] * cols + near, plane * cols + near).wait_recv())

        @pl.when(jnp.logical_not(is_mid))
        def _():
            @pl.loop(1, n)
            def _(k):
                block = lax.rem(me + k, n)
                sent_copy(c, 0, block, block).wait_recv()

    def back_out(c, action):
        @pl.when(is_mid)
        def _():
            for s in range(4):
                around(1, lambda near: act(
                    back_copy(c, hosted[s] * cols + near, s * cols + col, plane * cols + near), action))

        @pl.when(jnp.logical_not(is_mid))
        def _():
            for s in (0, 2, 3):
                around(0, lambda near: act(
                    back_copy(c, hosted[s] * cols + near, (4 + s) * cols + col, mid * cols + near), action))
            around(1, lambda near: act(
                back_copy(c, plane * cols + near, col, plane * cols + near), action))

    def back_start(c):
        back_out(c, "start")

        @pl.when(is_mid)
        def _():
            for s in range(4):
                home[c, s * cols + col] = got[c, hosted[s] * cols + col]

        @pl.when(jnp.logical_not(is_mid))
        def _():
            home[c, col] = got[c, me]

    def home_wait(c):
        @pl.when(is_mid)
        def _():
            for s in range(4):
                around(1, lambda near: back_copy(
                    c, 0, s * cols + near, plane * cols + near).wait_recv())
                if s != 1:
                    around(0, lambda near: back_copy(
                        c, 0, (4 + s) * cols + near, end * cols + near).wait_recv())

        @pl.when(jnp.logical_not(is_mid))
        def _():
            around(1, lambda near: back_copy(c, 0, near, plane * cols + near).wait_recv())

    def along_second(table, maps_of, cells_of):
        count = table.shape[0]

        @pl.loop(0, xs // 2)
        def _(h):
            halves = []
            for j in range(2):
                x = 2 * h + j
                cr, ci = maps_of(0, x).astype(F32), maps_of(1, x).astype(F32)
                vr, vi = cells_of(0, x).astype(F32), cells_of(1, x).astype(F32)
                halves.append(jnp.concatenate([cr * vr - ci * vi, cr * vi + ci * vr], axis=0).astype(BF16))
            lines = dot(table, jnp.concatenate(halves, axis=1))
            for j in range(2):
                rows[pl.ds(2 * h + j, count, stride=xs), :] = lines[:, j * nz:(j + 1) * nz]

    def own_maps(c):
        return (lambda p, x: sens[c, p, x]), (lambda p, x: image[p, x])

    def their_maps(c, s):
        return (lambda p, x: maps[s - 1, c, p, x]), (lambda p, x: images[s - 1, p, x])

    def pieces(count, first, place):
        for i in range(count):
            for q in range(2):
                place(i, q, slice((2 * i + q) * size, (2 * i + q + 1) * size), slice(q * part, (q + 1) * part))

    def half_place(i, s):
        return (lax.rem(i + 1 - half, 2) * 4 + s) * cols

    def fill_sent(c, count, start_of):
        def place(i, q, at, to):
            sent[c, pl.ds(start_of(i), cols), to, :] = rows[at, :].reshape(cols, part, nz).astype(BF16)
        pieces(count, 0, place)

    def fill_rows(c, count, start_of):
        def place(i, q, at, to):
            rows[at, :] = home[c, pl.ds(start_of(i), cols), to, :].reshape(size, nz).astype(F32)
        pieces(count, 0, place)

    def half_table():
        return fy[pl.ds(pl.multiple_of(half * 4 * wide, 4 * wide), 4 * wide), :]

    def plane_table():
        return fy[pl.ds(pl.multiple_of(plane * 2 * wide, 2 * wide), 2 * wide), :]

    def forward_half(c, s, sources):
        along_second(half_table(), *sources)
        fill_sent(c, 2, lambda i: half_place(i, s))

    def forward_plane(c, s, sources):
        along_second(plane_table(), *sources)
        fill_sent(c, 1, lambda i: s * cols)

    def forward_own(c):
        @pl.when(is_mid)
        def _():
            forward_half(c, 0, own_maps(c))
            keep_own(c, 0)
            forward_out(c, (0,), "start")

        @pl.when(jnp.logical_not(is_mid))
        def _():
            forward_plane(c, 0, own_maps(c))
            keep_own(c, 0)
            own_plane_out(c, 0, "start")

    def forward_near(c):
        forward_plane(c, 1, their_maps(c, 1))
        keep_own(c, 1)
        forward_out(c, (1,), "start")

    def forward_far(c):
        @pl.loop(2, 4)
        def _(s):
            forward_half(c, s, their_maps(c, s))

        for s in (2, 3):
            keep_own(c, s)
        forward_out(c, (2, 3), "start")

    def forward_last():
        along_second(fy[...], *own_maps(last))
        fill_sent(last, PLANES, lambda i: i * cols)
        all_traffic(sent_copy, "start")
        got[last, me] = sent[last, me]

    def middle(c):
        @pl.loop(0, kys // pair)
        def _(kp):
            base = pl.multiple_of(kp * 16, 16)
            cells = [got[c, :, pl.ds(q * part + base, 16), :].reshape(n * 16, nz) for q in range(2)]
            third = dot(jnp.concatenate(cells, axis=1), fzt[...]).reshape(n, pair, xs, 2 * gz)
            results = []
            for j in range(pair):
                b = third[:, j].reshape(nx, 2 * gz).astype(BF16)
                spectrum = dot(fx[...], jnp.concatenate([b[:, :gz], b[:, gz:]], axis=0))
                k = jnp.concatenate(
                    [filt[i, pl.ds(kp * pair + j, gx, stride=kys), :] for i in range(gz // 128)], axis=1)
                filtered = jnp.concatenate([spectrum[:gx] * k, spectrum[gx:] * k], axis=0).astype(BF16)
                first = dot(hx[...], filtered).astype(BF16)
                results.append(dot(jnp.concatenate([first[:nx], first[nx:]], axis=1), hzt[...]))
            for q in range(2):
                lines = [r[:, q * nz:(q + 1) * nz].reshape(n, 1, xs, nz) for r in results]
                got[c, :, pl.ds(q * part + base, 16), :] = (
                    jnp.concatenate(lines, axis=1).reshape(n, 16, nz).astype(BF16))

    def gather(table, maps_of, acc):
        count = table.shape[1]

        @pl.loop(0, xs // 2)
        def _(h):
            lines = [rows[pl.ds(2 * h + j, count, stride=xs), :] for j in range(2)]
            cells = dot(table, jnp.concatenate(lines, axis=1).astype(BF16))
            for j in range(2):
                x = 2 * h + j
                re, im = cells[:ny, j * nz:(j + 1) * nz], cells[ny:, j * nz:(j + 1) * nz]
                cr, ci = maps_of(0, x).astype(F32), maps_of(1, x).astype(F32)
                acc[0, x] = acc[0, x] + cr * re + ci * im
                acc[1, x] = acc[1, x] + cr * im - ci * re

    def half_back():
        return jnp.concatenate([hy[2 * half], hy[2 * half + 1]], axis=1)

    def inverse(c):
        home_wait(c)

        @pl.when(is_mid)
        def _():
            fill_rows(c, 2, lambda i: half_place(i, 0))
            gather(half_back(), own_maps(c)[0], out)
            fill_rows(c, 1, lambda i: cols)
            gather(hy[plane], their_maps(c, 1)[0], sums.at[0])

            @pl.loop(2, 4)
            def _(s):
                fill_rows(c, 2, lambda i: half_place(i, s))
                gather(half_back(), their_maps(c, s)[0], sums.at[s - 1])

        @pl.when(jnp.logical_not(is_mid))
        def _():
            fill_rows(c, 1, lambda i: 0)
            gather(hy[plane], own_maps(c)[0], out)

    def inverse_last():
        all_traffic(back_copy, "recv")
        fill_rows(last, PLANES, lambda i: i * cols)
        gather(jnp.concatenate([hy[i] for i in range(PLANES)], axis=1), own_maps(last)[0], out)

    def pass_on(c):
        map_copy(1, c).start()
        map_copy(0, c).wait_recv()
        map_copy(2, c).start()

    mine[...] = image[...].astype(BF16)

    @pl.when(is_mid)
    def _():
        image_copy(1).start()
        map_copy(1, 0).start()

    @pl.when(jnp.logical_not(is_mid))
    def _():
        image_copy(0).start()

        @pl.loop(0, last)
        def _(c):
            map_copy(0, c).start()

    @pl.when(me < n - 1)
    def _():
        for p in range(2):
            halo_copy(p, 0).start()

    @pl.when(me > 0)
    def _():
        for p in range(2):
            halo_copy(p, 1).start()

    sums[...] = jnp.zeros_like(sums)
    out[...] = jnp.zeros_like(out)
    forward_own(0)

    @pl.when(is_mid)
    def _():
        image_copy(0).wait_recv()
        image_copy(2).start()
        map_copy(0, 0).wait_recv()
        map_copy(2, 0).start()
        forward_near(0)
        pass_on(1)

    for copy in columns:
        copy.wait()

    @pl.loop(0, coils + 1)
    def _(t):
        @pl.when(jnp.logical_and(is_mid, t + 2 < last))
        def _():
            pass_on(t + 2)

        @pl.when(t + 1 < last)
        def _():
            forward_own(t + 1)

            @pl.when(is_mid)
            def _():
                forward_near(t + 1)

        @pl.when(t == coils - 3)
        def _():
            forward_last()

        @pl.when(jnp.logical_and(is_mid, t < last))
        def _():
            @pl.when(t == 0)
            def _():
                image_copy(1).wait_recv()
                image_copy(2).wait_recv()

            map_copy(1, t).wait_recv()
            map_copy(2, t).wait_recv()
            forward_far(t)

        @pl.when(t > 0)
        def _():
            c = t - 1

            @pl.when(c < last)
            def _():
                got_wait(c)

            @pl.when(c == last)
            def _():
                all_traffic(sent_copy, "recv")

            middle(c)

            @pl.when(c < last)
            def _():
                back_start(c)

            @pl.when(c == last)
            def _():
                all_traffic(back_copy, "start")
                home[last, me] = got[last, me]

        @pl.when(t > 1)
        def _():
            inverse(t - 2)

    @pl.when(is_mid)
    def _():
        parts[...] = sums[...].astype(BF16)
        for s in (2, 3, 1):
            total_copy(s).start()

    @pl.when(me < n - 1)
    def _():
        for p in range(2):
            halo_copy(p, 0).wait_send()
            halo_copy(p, 1).wait_recv()

    @pl.when(me > 0)
    def _():
        for p in range(2):
            halo_copy(p, 1).wait_send()
            halo_copy(p, 0).wait_recv()

    for p in range(2):
        for x in range(xs):
            here = image[p, x]
            if x == 0:
                before = jnp.where(me > 0, halo[0, p], 0.0)
            else:
                before = image[p, x - 1]
            if x == xs - 1:
                after = jnp.where(me < n - 1, halo[1, p], 0.0)
            else:
                after = image[p, x + 1]
            beside = before + after
            for axis in range(2):
                beside = beside + shifted(here, 1, axis) + shifted(here, -1, axis)
            out[p, x] = out[p, x] + smooth_weight * (6.0 * here - beside)

    inverse_last()
    total_copy(2).wait_recv()
    out[...] = out[...] + totals[0].astype(F32)

    @pl.when(jnp.logical_not(is_mid))
    def _():
        total_copy(3).wait_recv()
        out[...] = out[...] + totals[1].astype(F32)

    @pl.loop(0, last)
    def _(c):
        @pl.when(is_mid)
        def _():
            forward_out(c, (0, 1, 2, 3), "send")
            map_copy(1, c).wait_send()
            map_copy(2, c).wait_send()

        @pl.when(jnp.logical_not(is_mid))
        def _():
            own_plane_out(c, 0, "send")
            map_copy(0, c).wait_send()

        back_out(c, "send")

    all_traffic(sent_copy, "send")
    all_traffic(back_copy, "send")

    @pl.when(is_mid)
    def _():
        image_copy(1).wait_send()
        image_copy(2).wait_send()
        for s in (1, 2, 3):
            total_copy(s).wait_send()

    @pl.when(jnp.logical_not(is_mid))
    def _():
        image_copy(0).wait_send()


def fused(n, image, sensitivity, kernel):
    coils, _, xs, ny, nz = sensitivity.shape
    gx, kys, gz = kernel.shape
    nx, gy = n * xs, n * kys
    cols, wide = n // PLANES, gy // PLANES
    block = (2 * kys * xs, nz)
    forward = factor(gy, ny, gy, -1.0).reshape(2, PLANES, wide, 2 * ny)
    backward = factor(ny, gy, gy, 1.0).reshape(2 * ny, 2, PLANES, wide)
    tables = (
        forward.transpose(1, 0, 2, 3).reshape(2 * gy, 2 * ny),
        factor(gz, nz, gz, -1.0).T,
        factor(gx, nx, gx, -1.0),
        factor(nx, gx, gx, 1.0),
        factor(nz, gz, gz, 1.0).T,
        backward.transpose(2, 0, 1, 3).reshape(PLANES, 2 * ny, 2 * wide),
    )
    vmem = pl.BlockSpec(memory_space=pltpu.VMEM)
    dma = pltpu.SemaphoreType.DMA
    slots = 2 * PLANES * cols
    slab = image.shape
    return pl.pallas_call(
        functools.partial(kernel_body, n),
        out_shape=jax.ShapeDtypeStruct(image.shape, F32),
        in_specs=[vmem] * 2 + [pl.BlockSpec(memory_space=pl.ANY)] + [vmem] * 6,
        out_specs=vmem,
        scratch_shapes=[
            pltpu.VMEM((coils, slots, *block), BF16),
            pltpu.VMEM((coils, n, *block), BF16),
            pltpu.VMEM((coils, slots, *block), BF16),
            pltpu.VMEM((2 * gy * xs, nz), F32),
            pltpu.VMEM((2, 2, ny, nz), F32),
            pltpu.VMEM((gz // 128, gx * kys, 128), F32),
            pltpu.VMEM((3, coils - 1, *slab), BF16),
            pltpu.VMEM((3, *slab), BF16),
            pltpu.VMEM(slab, BF16),
            pltpu.VMEM((3, *slab), F32),
            pltpu.VMEM((3, *slab), BF16),
            pltpu.VMEM((2, *slab), BF16),
            dma((coils, slots)), dma((coils, n)), dma((coils, n)), dma((coils, slots)),
            dma((2, 2)), dma((2, 2)), dma((gz // 128,)),
            dma((3, coils)), dma((3, coils)), dma((3,)), dma((3,)), dma((3,)), dma((2,)),
        ],
        compiler_params=pltpu.CompilerParams(
            collective_id=0, has_side_effects=True, vmem_limit_bytes=63 * 2**20),
    )(image, sensitivity, kernel.reshape(gx * kys, gz), *[jnp.asarray(t) for t in tables])


def with_halo(cells, axis, dim):
    count = lax.axis_size(axis)
    head = lax.slice_in_dim(cells, 0, 1, axis=dim)
    tail = lax.slice_in_dim(cells, cells.shape[dim] - 1, cells.shape[dim], axis=dim)
    return jnp.concatenate(
        [
            lax.ppermute(tail, axis, [(i, i + 1) for i in range(count - 1)]),
            cells,
            lax.ppermute(head, axis, [(i + 1, i) for i in range(count - 1)]),
        ],
        axis=dim,
    )


def staged(n, image, sensitivity, kernel):
    coils, _, xs, ny, nz = sensitivity.shape
    gx, kys, gz = kernel.shape
    nx, gy = n * xs, n * kys

    def table(count_out, count_in, length, sign_value):
        both = factor(count_out, count_in, length, sign_value)
        return jnp.asarray(both.reshape(2, count_out, 2, count_in).transpose(0, 2, 1, 3))

    def apply(matrix, values, pattern):
        return jnp.einsum(pattern, matrix, values, preferred_element_type=F32)

    real, imag = sensitivity[:, 0].astype(F32), sensitivity[:, 1].astype(F32)
    images = jnp.stack(
        [real * image[0] - imag * image[1], real * image[1] + imag * image[0]], axis=1).astype(BF16)
    second = apply(table(gy, ny, gy, -1.0), images, "pqkj,cqajb->cpakb").astype(BF16)
    second = lax.all_to_all(second, "slab", split_axis=3, concat_axis=2, tiled=True)
    third = apply(table(gz, nz, gz, -1.0), second, "pqkj,cqabj->cpabk").astype(BF16)
    spectrum = apply(table(gx, nx, gx, -1.0), third, "pqkj,cqjab->cpkab")
    filtered = (spectrum * kernel).astype(BF16)
    first = apply(table(nx, gx, gx, 1.0), filtered, "pqkj,cqjab->cpkab").astype(BF16)
    back = apply(table(nz, gz, gz, 1.0), first, "pqkj,cqabj->cpabk").astype(BF16)
    back = lax.all_to_all(back, "slab", split_axis=2, concat_axis=3, tiled=True)
    cells = apply(table(ny, gy, gy, 1.0), back, "pqkj,cqajb->cpakb")
    summed = jnp.stack([
        jnp.sum(real * cells[:, 0] + imag * cells[:, 1], axis=0),
        jnp.sum(real * cells[:, 1] - imag * cells[:, 0], axis=0)])
    padded = with_halo(image.astype(BF16), "slab", 1).astype(image.dtype)
    beside = padded[:, 2:] + padded[:, :-2]
    wide = jnp.pad(image, ((0, 0), (0, 0), (1, 1), (1, 1)))
    beside = beside + wide[:, :, 2:, 1:-1] + wide[:, :, :-2, 1:-1]
    beside = beside + wide[:, :, 1:-1, 2:] + wide[:, :, 1:-1, :-2]
    return summed + smooth_weight * (6.0 * image - beside)


def solution(mesh):
    n = mesh.shape["slab"]

    def local(image, sensitivity, kernel):
        tiled = sensitivity.shape[2] == 8 and kernel.shape[1] % 2 == 0 and n % PLANES == 0 and sensitivity.shape[0] == 6
        form = fused if tiled else staged
        return form(n, image, sensitivity, kernel)

    return jax.shard_map(
        local,
        mesh=mesh,
        in_specs=(
            P(None, "slab", "scan", None),
            P("scan", None, "slab", None, None),
            P(None, "slab", None),
        ),
        out_specs=P(None, "slab", "scan", None),
        check_vma=False,
    )
```

time: 290 us -> 280 us (0.966)
  Pallas kernels: 288 us -> 277 us
    pallas_call x1, Pallas kernels: 288 us -> 277 us  [fused(): pl.pallas_call(functools.partial(kernel_body, n), out_shape=jax.ShapeDtyp...]
where the time goes in v1:
time: 280 us; the launch traced here: 279 us
  Pallas kernels  277 us (99%)
    pallas_call x1, Pallas kernels, fused(): pl.pallas_call(functools.partial(kernel_body, n), out_shape=jax.ShapeDtyp...  277 us

profile of v1, /device:TPU:27, one launch (start us, length us, event | category | flops | bytes accessed | tf_op | source)
XLA Modules:
  0.0 279.4 jit_solution(6734938243308778805)
XLA Ops:
  0.0 277.1 %shard_map.91 = f32[2,8,128,128]{3,2,1,0:T(8,128)} custom-call(f32[2,8,128,128]{3,2,1,0:T(8,128)} %image.1, bf16[6,2,8,128,128]{4,3,2,1,0:T(8,128)(2,1)} %sens.1, f32[4096,256]{1,0:T(8,128)} %bitcast.1, bf16[512,256]{1,0:T(8,128)(2,1)} %constant.8.clone.fy, bf16[256,512]{1,0:T(8,128)(2,1)} %constant.9.clone.fzt.hx, bf16[512,256]{1,0:T(8,128)(2,1)} %constant.10.clone.fx.hzt, ...), custom_call_target="tpu_custom_call" | custom-call | tf_op jit(solution)/shard_map/pallas_call | solution.py:545
  277.1 2.3 copy.11

commit v2 on v1

--- a/solution.py
+++ b/solution.py
@@ -35,11 +35,25 @@
 
 
 PLANES = 4
+MID_ORDER = (
+    ("map", 0), ("mapn", 0), ("img", 0), ("mapn", 3), ("fo", 1), ("map", 1), ("pass", 0), ("imgp", 0),
+    ("mapn", 1), ("fl", 0), ("fn", 0), ("pass", 1), ("map", 2), ("fn", 1), ("mapn", 2), ("fo", 0),
+    ("imgw", 0), ("ff", 0), ("pass", 2), ("fo", 3), ("fo", 4), ("fo", 2), ("map", 3), ("pass", 3), ("fn", 2),
+    ("fn", 3), ("wt", 0), ("mid", 0), ("ff", 1), ("ff", 2), ("mapn", 4), ("mid", 1), ("map", 4), ("pass", 4),
+    ("inv", 0), ("ff", 3), ("flf", 0), ("mid", 2), ("ff", 4), ("mid", 3), ("fn", 4), ("mid", 5), ("inv", 2),
+    ("inv", 1), ("inv", 3), ("mid", 4), ("inv", 4),
+)
+END_ORDER = (
+    ("mapn", 0), ("img", 0), ("fo", 0), ("mapn", 3), ("fl", 0), ("mapn", 1), ("imgw", 0), ("fn", 1),
+    ("fo", 4), ("fo", 3), ("fn", 3), ("mapn", 2), ("fo", 2), ("mapn", 4), ("fo", 1), ("fn", 0), ("wt", 0),
+    ("mid", 0), ("mid", 1), ("flf", 0), ("inv", 0), ("fn", 2), ("mid", 3), ("fn", 4), ("mid", 2), ("mid", 4),
+    ("mid", 5), ("inv", 1), ("inv", 2), ("inv", 3), ("inv", 4),
+)
 
 
 def kernel_body(
     n, image, sens, weight, fy, fzt, fx, hx, hzt, hy, out,
-    sent, got, home, rows, halo, filt, maps, images, mine, sums, parts, totals,
+    sent, got, home, rows, halo, filt, spread, maps, images, mine, sums, parts, totals,
     send1, recv1, send2, recv2, hsend, hrecv, wsem, msend, mrecv, isend, irecv, tsend, trecv,
 ):
     me = lax.axis_index("slab")
@@ -57,8 +71,21 @@
     half = plane // 2
     end, mid = 3 * half, 1 + half
     other_mid, other_end = 2 - half, 3 - 3 * half
-    hosted = (mid, end, other_mid, other_end)
     is_mid = plane == mid
+    near_plane = jnp.where(is_mid, end, mid)
+    nh = n // 2
+    place = lax.rem(me, nh)
+
+    def plane_of(s):
+        if isinstance(s, int):
+            return (plane, near_plane, other_mid, other_end)[s]
+        return jnp.where(s == 2, other_mid, other_end)
+
+    def if_mid(body):
+        pl.when(is_mid)(body)
+
+    def if_end(body):
+        pl.when(jnp.logical_not(is_mid))(body)
 
     columns = [
         pltpu.make_async_copy(weight.at[:, pl.ds(i * 128, 128)], filt.at[i], wsem.at[i])
@@ -86,20 +113,20 @@
         return remote(image.at[p, edge], halo.at[side, p], hsend.at[side, p], hrecv.at[side, p],
                       lax.rem(to + n, n))
 
-    def map_copy(kind, c):
-        source = maps.at[0, c] if kind == 2 else sens.at[c]
-        to = (mid if kind == 0 else other_mid) * cols + col
-        return remote(source, maps.at[kind, c], msend.at[kind, c], mrecv.at[kind, c], to)
-
-    def image_copy(kind):
-        source = images.at[0] if kind == 2 else mine
-        to = (mid if kind == 0 else other_mid) * cols + col
-        return remote(source, images.at[kind], isend.at[kind], irecv.at[kind], to)
-
-    def total_copy(slot):
-        landing = 1 if slot == 3 else 0
-        return remote(parts.at[slot - 1], totals.at[landing], tsend.at[slot - 1], trecv.at[landing],
-                      hosted[slot] * cols + col)
+    def map_copy(s, c):
+        source = maps.at[0, c] if isinstance(s, int) and s == 3 else sens.at[c]
+        to = (near_plane if isinstance(s, int) and s == 1 else other_mid) * cols + col
+        return remote(source, maps.at[s - 1, c], msend.at[s - 1, c], mrecv.at[s - 1, c], to)
+
+    def image_copy(s):
+        source = images.at[0] if s == 3 else mine
+        to = (near_plane if s == 1 else other_mid) * cols + col
+        return remote(source, images.at[s - 1], isend.at[s - 1], irecv.at[s - 1], to)
+
+    def total_copy(s):
+        landing = 1 if isinstance(s, int) and s == 1 else 0
+        return remote(parts.at[s - 1], totals.at[landing], tsend.at[s - 1], trecv.at[landing],
+                      plane_of(s) * cols + col)
 
     def act(copy, action):
         if action == "start":
@@ -120,89 +147,76 @@
     def back_copy(c, slot, landing, to):
         return remote(got.at[c, slot], home.at[c, landing], send2.at[c, slot], recv2.at[c, landing], to)
 
-    def all_traffic(copy_of, action):
-        @pl.loop(1, n)
+    def near_half(copy_of, action):
+        @pl.loop(1, nh)
         def _(k):
-            to = lax.rem(me + k, n)
+            to = half * nh + lax.rem(place + k, nh)
             act(copy_of(last, to, to if action == "recv" else me, to), action)
 
+    def far_half(copy_of, action):
+        @pl.loop(0, nh)
+        def _(k):
+            to = (1 - half) * nh + lax.rem(place + k, nh)
+            act(copy_of(last, to, to if action == "recv" else me, to), action)
+
     def own_plane_out(c, s, action):
-        block = (plane if s == 0 else hosted[s]) * cols + col
         around(1, lambda near: act(
-            sent_copy(c, s * cols + near, block, plane * cols + near), action))
+            sent_copy(c, s * cols + near, plane_of(s) * cols + col, plane * cols + near), action))
 
     def end_plane_out(c, s, action):
         around(0, lambda near: act(
-            sent_copy(c, (4 + s) * cols + near, hosted[s] * cols + col, end * cols + near), action))
+            sent_copy(c, (2 + s) * cols + near, plane_of(s) * cols + col, end * cols + near), action))
 
     def keep_own(c, s):
-        got[c, (plane if s == 0 else hosted[s]) * cols + col] = sent[c, s * cols + col]
-
-    def forward_out(c, slots, action):
-        for s in slots:
-            own_plane_out(c, s, action)
-            if s != 1:
-                end_plane_out(c, s, action)
+        got[c, plane_of(s) * cols + col] = sent[c, s * cols + col]
 
     def got_wait(c):
-        @pl.when(is_mid)
-        def _():
-            for s in range(4):
-                around(1, lambda near: sent_copy(
-                    c, near, hosted[s] * cols + near, plane * cols + near).wait_recv())
-
-        @pl.when(jnp.logical_not(is_mid))
-        def _():
-            @pl.loop(1, n)
-            def _(k):
-                block = lax.rem(me + k, n)
-                sent_copy(c, 0, block, block).wait_recv()
+        for s in range(4):
+            around(1, lambda near: sent_copy(
+                c, near, plane_of(s) * cols + near, plane * cols + near).wait_recv())
+
+        @if_end
+        def _():
+            for s in (2, 3):
+                sent_copy(c, col, plane_of(s) * cols + col, mid * cols + col).wait_recv()
 
     def back_out(c, action):
-        @pl.when(is_mid)
-        def _():
-            for s in range(4):
-                around(1, lambda near: act(
-                    back_copy(c, hosted[s] * cols + near, s * cols + col, plane * cols + near), action))
-
-        @pl.when(jnp.logical_not(is_mid))
-        def _():
-            for s in (0, 2, 3):
-                around(0, lambda near: act(
-                    back_copy(c, hosted[s] * cols + near, (4 + s) * cols + col, mid * cols + near), action))
+        def within(s):
             around(1, lambda near: act(
-                back_copy(c, plane * cols + near, col, plane * cols + near), action))
+                back_copy(c, plane_of(s) * cols + near, s * cols + col, plane * cols + near), action))
+
+        def across(s):
+            around(0, lambda near: act(
+                back_copy(c, plane_of(s) * cols + near, (2 + s) * cols + col, mid * cols + near), action))
+
+        for s in (3, 2):
+            if_mid(functools.partial(within, s))
+            if_end(functools.partial(across, s))
+        for s in (1, 0):
+            within(s)
 
     def back_start(c):
         back_out(c, "start")
 
-        @pl.when(is_mid)
-        def _():
-            for s in range(4):
-                home[c, s * cols + col] = got[c, hosted[s] * cols + col]
-
-        @pl.when(jnp.logical_not(is_mid))
-        def _():
-            home[c, col] = got[c, me]
-
-    def home_wait(c):
-        @pl.when(is_mid)
-        def _():
-            for s in range(4):
-                around(1, lambda near: back_copy(
-                    c, 0, s * cols + near, plane * cols + near).wait_recv())
-                if s != 1:
-                    around(0, lambda near: back_copy(
-                        c, 0, (4 + s) * cols + near, end * cols + near).wait_recv())
-
-        @pl.when(jnp.logical_not(is_mid))
-        def _():
-            around(1, lambda near: back_copy(c, 0, near, plane * cols + near).wait_recv())
+        @if_mid
+        def _():
+            for s in (3, 2):
+                home[c, s * cols + col] = got[c, plane_of(s) * cols + col]
+
+        for s in (1, 0):
+            home[c, s * cols + col] = got[c, plane_of(s) * cols + col]
+
+    def home_wait(c, s):
+        around(1, lambda near: back_copy(c, 0, s * cols + near, plane * cols + near).wait_recv())
+
+    def far_home_wait(c, s):
+        home_wait(c, s)
+        around(0, lambda near: back_copy(c, 0, (2 + s) * cols + near, end * cols + near).wait_recv())
 
     def along_second(table, maps_of, cells_of):
         count = table.shape[0]
 
-        @pl.loop(0, xs // 2)
+        @pl.loop(0, xs // 2, unroll=xs // 2)
         def _(h):
             halves = []
             for j in range(2):
@@ -226,7 +240,7 @@
                 place(i, q, slice((2 * i + q) * size, (2 * i + q + 1) * size), slice(q * part, (q + 1) * part))
 
     def half_place(i, s):
-        return (lax.rem(i + 1 - half, 2) * 4 + s) * cols
+        return (lax.rem(i + 1 - half, 2) * 2 + s) * cols
 
     def fill_sent(c, count, start_of):
         def place(i, q, at, to):
@@ -253,37 +267,33 @@
         fill_sent(c, 1, lambda i: s * cols)
 
     def forward_own(c):
-        @pl.when(is_mid)
-        def _():
-            forward_half(c, 0, own_maps(c))
-            keep_own(c, 0)
-            forward_out(c, (0,), "start")
-
-        @pl.when(jnp.logical_not(is_mid))
-        def _():
-            forward_plane(c, 0, own_maps(c))
-            keep_own(c, 0)
-            own_plane_out(c, 0, "start")
+        forward_plane(c, 0, own_maps(c))
+        keep_own(c, 0)
+        own_plane_out(c, 0, "start")
 
     def forward_near(c):
+        if_end(lambda: map_copy(1, c).wait_recv())
         forward_plane(c, 1, their_maps(c, 1))
         keep_own(c, 1)
-        forward_out(c, (1,), "start")
+        own_plane_out(c, 1, "start")
 
     def forward_far(c):
         @pl.loop(2, 4)
         def _(s):
+            map_copy(s, c).wait_recv()
             forward_half(c, s, their_maps(c, s))
-
-        for s in (2, 3):
             keep_own(c, s)
-        forward_out(c, (2, 3), "start")
-
-    def forward_last():
+            own_plane_out(c, s, "start")
+            end_plane_out(c, s, "start")
+
+    def forward_last(c):
         along_second(fy[...], *own_maps(last))
         fill_sent(last, PLANES, lambda i: i * cols)
-        all_traffic(sent_copy, "start")
+        near_half(sent_copy, "start")
         got[last, me] = sent[last, me]
+
+    def forward_last_far(c):
+        far_half(sent_copy, "start")
 
     def middle(c):
         @pl.loop(0, kys // pair)
@@ -291,15 +301,17 @@
             base = pl.multiple_of(kp * 16, 16)
             cells = [got[c, :, pl.ds(q * part + base, 16), :].reshape(n * 16, nz) for q in range(2)]
             third = dot(jnp.concatenate(cells, axis=1), fzt[...]).reshape(n, pair, xs, 2 * gz)
-            results = []
-            for j in range(pair):
-                b = third[:, j].reshape(nx, 2 * gz).astype(BF16)
-                spectrum = dot(fx[...], jnp.concatenate([b[:, :gz], b[:, gz:]], axis=0))
-                k = jnp.concatenate(
-                    [filt[i, pl.ds(kp * pair + j, gx, stride=kys), :] for i in range(gz // 128)], axis=1)
-                filtered = jnp.concatenate([spectrum[:gx] * k, spectrum[gx:] * k], axis=0).astype(BF16)
-                first = dot(hx[...], filtered).astype(BF16)
-                results.append(dot(jnp.concatenate([first[:nx], first[nx:]], axis=1), hzt[...]))
+            halves = [third[:, j].reshape(nx, 2 * gz).astype(BF16) for j in range(pair)]
+            spectrum = dot(fx[...], jnp.concatenate(
+                [jnp.concatenate([b[:, q * gz:(q + 1) * gz] for b in halves], axis=1) for q in range(2)],
+                axis=0))
+            k = jnp.concatenate([spread[kp * pair + j] for j in range(pair)], axis=1)
+            filtered = jnp.concatenate([spectrum[:gx] * k, spectrum[gx:] * k], axis=0).astype(BF16)
+            first = dot(hx[...], filtered).astype(BF16)
+            both = dot(jnp.concatenate(
+                [jnp.concatenate([first[:nx, j * gz:(j + 1) * gz], first[nx:, j * gz:(j + 1) * gz]], axis=1)
+                 for j in range(pair)], axis=0), hzt[...])
+            results = [both[j * nx:(j + 1) * nx] for j in range(pair)]
             for q in range(2):
                 lines = [r[:, q * nz:(q + 1) * nz].reshape(n, 1, xs, nz) for r in results]
                 got[c, :, pl.ds(q * part + base, 16), :] = (
@@ -308,7 +320,7 @@
     def gather(table, maps_of, acc):
         count = table.shape[1]
 
-        @pl.loop(0, xs // 2)
+        @pl.loop(0, xs // 2, unroll=xs // 2)
         def _(h):
             lines = [rows[pl.ds(2 * h + j, count, stride=xs), :] for j in range(2)]
             cells = dot(table, jnp.concatenate(lines, axis=1).astype(BF16))
@@ -322,50 +334,97 @@
     def half_back():
         return jnp.concatenate([hy[2 * half], hy[2 * half + 1]], axis=1)
 
+    def return_total(c, s):
+        @pl.when(c == last - 1)
+        def _():
+            parts[s - 1] = sums[s - 1].astype(BF16)
+            total_copy(s).start()
+
     def inverse(c):
-        home_wait(c)
-
-        @pl.when(is_mid)
-        def _():
-            fill_rows(c, 2, lambda i: half_place(i, 0))
-            gather(half_back(), own_maps(c)[0], out)
-            fill_rows(c, 1, lambda i: cols)
-            gather(hy[plane], their_maps(c, 1)[0], sums.at[0])
-
-            @pl.loop(2, 4)
-            def _(s):
+        @if_mid
+        def _():
+            @pl.loop(0, 2)
+            def _(k):
+                s = 3 - k
+                far_home_wait(c, s)
                 fill_rows(c, 2, lambda i: half_place(i, s))
                 gather(half_back(), their_maps(c, s)[0], sums.at[s - 1])
-
-        @pl.when(jnp.logical_not(is_mid))
-        def _():
-            fill_rows(c, 1, lambda i: 0)
-            gather(hy[plane], own_maps(c)[0], out)
+                return_total(c, s)
+
+        home_wait(c, 1)
+        fill_rows(c, 1, lambda i: cols)
+        gather(hy[plane], their_maps(c, 1)[0], sums.at[0])
+        return_total(c, 1)
+        home_wait(c, 0)
+        fill_rows(c, 1, lambda i: 0)
+        gather(hy[plane], own_maps(c)[0], out)
 
     def inverse_last():
-        all_traffic(back_copy, "recv")
+        near_half(back_copy, "recv")
+        far_half(back_copy, "recv")
         fill_rows(last, PLANES, lambda i: i * cols)
         gather(jnp.concatenate([hy[i] for i in range(PLANES)], axis=1), own_maps(last)[0], out)
 
-    def pass_on(c):
-        map_copy(1, c).start()
-        map_copy(0, c).wait_recv()
-        map_copy(2, c).start()
+    def pass_map(c):
+        map_copy(1, c).wait_recv()
+        map_copy(3, c).start()
+
+    def pass_image(c):
+        image_copy(1).wait_recv()
+        image_copy(3).start()
+
+    def await_image(c):
+        if_end(lambda: image_copy(1).wait_recv())
+
+        @if_mid
+        def _():
+            image_copy(2).wait_recv()
+            image_copy(3).wait_recv()
+
+    def start_image(c):
+        image_copy(1).start()
+        if_mid(lambda: image_copy(2).start())
+
+    def whole_middle(c):
+        @pl.when(c < last)
+        def _():
+            got_wait(c)
+
+        @pl.when(c == last)
+        def _():
+            near_half(sent_copy, "recv")
+            far_half(sent_copy, "recv")
+
+        middle(c)
+
+        @pl.when(c < last)
+        def _():
+            back_start(c)
+
+        @pl.when(c == last)
+        def _():
+            far_half(back_copy, "start")
+            near_half(back_copy, "start")
+            home[last, me] = got[last, me]
+
+    def spread_filter(c):
+        for copy in columns:
+            copy.wait()
+
+        @pl.loop(0, kys)
+        def _(ky):
+            for i in range(gz // 128):
+                spread[ky, :, i * 128:(i + 1) * 128] = filt[i, pl.ds(ky, gx, stride=kys), :]
+
+    steps = {
+        "wt": spread_filter,
+        "img": start_image, "imgp": pass_image, "imgw": await_image,
+        "map": lambda c: map_copy(2, c).start(), "mapn": lambda c: map_copy(1, c).start(),
+        "pass": pass_map, "fo": forward_own, "fn": forward_near, "ff": forward_far,
+        "fl": forward_last, "flf": forward_last_far, "mid": whole_middle, "inv": inverse,
+    }
 
     mine[...] = image[...].astype(BF16)
-
-    @pl.when(is_mid)
-    def _():
-        image_copy(1).start()
-        map_copy(1, 0).start()
-
-    @pl.when(jnp.logical_not(is_mid))
-    def _():
-        image_copy(0).start()
-
-        @pl.loop(0, last)
-        def _(c):
-            map_copy(0, c).start()
 
     @pl.when(me < n - 1)
     def _():
@@ -379,81 +438,15 @@
 
     sums[...] = jnp.zeros_like(sums)
     out[...] = jnp.zeros_like(out)
-    forward_own(0)
-
-    @pl.when(is_mid)
-    def _():
-        image_copy(0).wait_recv()
-        image_copy(2).start()
-        map_copy(0, 0).wait_recv()
-        map_copy(2, 0).start()
-        forward_near(0)
-        pass_on(1)
-
-    for copy in columns:
-        copy.wait()
-
-    @pl.loop(0, coils + 1)
+    @pl.loop(0, max(len(MID_ORDER), len(END_ORDER)))
     def _(t):
-        @pl.when(jnp.logical_and(is_mid, t + 2 < last))
-        def _():
-            pass_on(t + 2)
-
-        @pl.when(t + 1 < last)
-        def _():
-            forward_own(t + 1)
-
-            @pl.when(is_mid)
-            def _():
-                forward_near(t + 1)
-
-        @pl.when(t == coils - 3)
-        def _():
-            forward_last()
-
-        @pl.when(jnp.logical_and(is_mid, t < last))
-        def _():
-            @pl.when(t == 0)
-            def _():
-                image_copy(1).wait_recv()
-                image_copy(2).wait_recv()
-
-            map_copy(1, t).wait_recv()
-            map_copy(2, t).wait_recv()
-            forward_far(t)
-
-        @pl.when(t > 0)
-        def _():
-            c = t - 1
-
-            @pl.when(c < last)
-            def _():
-                got_wait(c)
-
-            @pl.when(c == last)
-            def _():
-                all_traffic(sent_copy, "recv")
-
-            middle(c)
-
-            @pl.when(c < last)
-            def _():
-                back_start(c)
-
-            @pl.when(c == last)
-            def _():
-                all_traffic(back_copy, "start")
-                home[last, me] = got[last, me]
-
-        @pl.when(t > 1)
-        def _():
-            inverse(t - 2)
-
-    @pl.when(is_mid)
-    def _():
-        parts[...] = sums[...].astype(BF16)
-        for s in (2, 3, 1):
-            total_copy(s).start()
+        for name, body in steps.items():
+            chosen = [
+                sum(jnp.where(t == i, c + 1, 0) for i, (other, c) in enumerate(order) if other == name)
+                for order in (MID_ORDER, END_ORDER)
+            ]
+            code = jnp.where(is_mid, *chosen)
+            pl.when(code > 0)(functools.partial(body, code - 1))
 
     @pl.when(me < n - 1)
     def _():
@@ -484,42 +477,36 @@
             out[p, x] = out[p, x] + smooth_weight * (6.0 * here - beside)
 
     inverse_last()
+    total_copy(1).wait_recv()
     total_copy(2).wait_recv()
-    out[...] = out[...] + totals[0].astype(F32)
-
-    @pl.when(jnp.logical_not(is_mid))
-    def _():
-        total_copy(3).wait_recv()
-        out[...] = out[...] + totals[1].astype(F32)
+    out[...] = out[...] + totals[0].astype(F32) + totals[1].astype(F32)
 
     @pl.loop(0, last)
     def _(c):
-        @pl.when(is_mid)
-        def _():
-            forward_out(c, (0, 1, 2, 3), "send")
-            map_copy(1, c).wait_send()
-            map_copy(2, c).wait_send()
-
-        @pl.when(jnp.logical_not(is_mid))
-        def _():
-            own_plane_out(c, 0, "send")
-            map_copy(0, c).wait_send()
+        for s in range(2):
+            own_plane_out(c, s, "send")
+        map_copy(1, c).wait_send()
+
+        @if_mid
+        def _():
+            for s in (2, 3):
+                own_plane_out(c, s, "send")
+                end_plane_out(c, s, "send")
+                map_copy(s, c).wait_send()
 
         back_out(c, "send")
 
-    all_traffic(sent_copy, "send")
-    all_traffic(back_copy, "send")
-
-    @pl.when(is_mid)
+    for copy_of in (sent_copy, back_copy):
+        near_half(copy_of, "send")
+        far_half(copy_of, "send")
+    image_copy(1).wait_send()
+    total_copy(1).wait_send()
+
+    @if_mid
     def _():
-        image_copy(1).wait_send()
-        image_copy(2).wait_send()
-        for s in (1, 2, 3):
+        for s in (2, 3):
+            image_copy(s).wait_send()
             total_copy(s).wait_send()
-
-    @pl.when(jnp.logical_not(is_mid))
-    def _():
-        image_copy(0).wait_send()
 
 
 def fused(n, image, sensitivity, kernel):
@@ -540,7 +527,7 @@
     )
     vmem = pl.BlockSpec(memory_space=pltpu.VMEM)
     dma = pltpu.SemaphoreType.DMA
-    slots = 2 * PLANES * cols
+    slots = (PLANES + 2) * cols
     slab = image.shape
     return pl.pallas_call(
         functools.partial(kernel_body, n),
@@ -554,6 +541,7 @@
             pltpu.VMEM((2 * gy * xs, nz), F32),
             pltpu.VMEM((2, 2, ny, nz), F32),
             pltpu.VMEM((gz // 128, gx * kys, 128), F32),
+            pltpu.VMEM((kys, gx, gz), F32),
             pltpu.VMEM((3, coils - 1, *slab), BF16),
             pltpu.VMEM((3, *slab), BF16),
             pltpu.VMEM(slab, BF16),

time: 280 us -> 247 us (0.88)
  Pallas kernels: 277 us -> 242 us
    pallas_call x1, Pallas kernels: 277 us -> 242 us  [fused(): pl.pallas_call(functools.partial(kernel_body, n), out_shape=jax.ShapeDtyp...]
where the time goes in v2:
time: 247 us; the launch traced here: 244 us
  Pallas kernels  242 us (98%)
    pallas_call x1, Pallas kernels, fused(): pl.pallas_call(functools.partial(kernel_body, n), out_shape=jax.ShapeDtyp...  242 us

profile of v2, /device:TPU:27, one launch (start us, length us, event | category | flops | bytes accessed | tf_op | source)
XLA Modules:
  0.0 244.5 jit_solution(15533460031899560839)
XLA Ops:
  0.0 242.2 %shard_map.91 = f32[2,8,128,128]{3,2,1,0:T(8,128)} custom-call(f32[2,8,128,128]{3,2,1,0:T(8,128)} %image.1, bf16[6,2,8,128,128]{4,3,2,1,0:T(8,128)(2,1)} %sens.1, f32[4096,256]{1,0:T(8,128)} %bitcast.1, bf16[512,256]{1,0:T(8,128)(2,1)} %constant.8.clone.fy, bf16[256,512]{1,0:T(8,128)(2,1)} %constant.9.clone.fzt.hx, bf16[512,256]{1,0:T(8,128)(2,1)} %constant.10.clone.fx.hzt, ...), custom_call_target="tpu_custom_call" | custom-call | tf_op jit(solution)/shard_map/pallas_call | solution.py:532
  242.2 2.3 copy.11

commit v3 on v2

--- a/solution.py
+++ b/solution.py
@@ -36,26 +36,27 @@
 
 PLANES = 4
 MID_ORDER = (
-    ("map", 0), ("mapn", 0), ("img", 0), ("mapn", 3), ("fo", 1), ("map", 1), ("pass", 0), ("imgp", 0),
-    ("mapn", 1), ("fl", 0), ("fn", 0), ("pass", 1), ("map", 2), ("fn", 1), ("mapn", 2), ("fo", 0),
-    ("imgw", 0), ("ff", 0), ("pass", 2), ("fo", 3), ("fo", 4), ("fo", 2), ("map", 3), ("pass", 3), ("fn", 2),
-    ("fn", 3), ("wt", 0), ("mid", 0), ("ff", 1), ("ff", 2), ("mapn", 4), ("mid", 1), ("map", 4), ("pass", 4),
-    ("inv", 0), ("ff", 3), ("flf", 0), ("mid", 2), ("ff", 4), ("mid", 3), ("fn", 4), ("mid", 5), ("inv", 2),
-    ("inv", 1), ("inv", 3), ("mid", 4), ("inv", 4),
+    ("map", 0), ("img", 0), ("mapn", 0), ("fo", 0), ("fo", 1), ("fo", 2), ("fo", 3), ("fo", 4), ("mapn", 1),
+    ("map", 1), ("mapn", 2), ("pass", 0), ("imgp", 0), ("fn", 0), ("pass", 1), ("fn", 1), ("map", 2),
+    ("mapn", 3), ("imgw", 0), ("ff", 0), ("fl", 0), ("pass", 2), ("fn", 2), ("map", 3), ("mapn", 4),
+    ("ff", 1), ("pass", 3), ("fn", 3), ("wt", 0), ("mid", 0), ("map", 4), ("ff", 2), ("mid", 1), ("pass", 4),
+    ("fn", 4), ("inv", 0), ("ff", 3), ("mid", 2), ("flf", 0), ("ff", 4), ("mid", 3), ("mid", 4), ("inv", 1),
+    ("mid", 5), ("inv", 2), ("inv", 3), ("inv", 4),
 )
 END_ORDER = (
-    ("mapn", 0), ("img", 0), ("fo", 0), ("mapn", 3), ("fl", 0), ("mapn", 1), ("imgw", 0), ("fn", 1),
-    ("fo", 4), ("fo", 3), ("fn", 3), ("mapn", 2), ("fo", 2), ("mapn", 4), ("fo", 1), ("fn", 0), ("wt", 0),
-    ("mid", 0), ("mid", 1), ("flf", 0), ("inv", 0), ("fn", 2), ("mid", 3), ("fn", 4), ("mid", 2), ("mid", 4),
-    ("mid", 5), ("inv", 1), ("inv", 2), ("inv", 3), ("inv", 4),
+    ("img", 0), ("mapn", 0), ("fo", 0), ("fo", 1), ("mapn", 1), ("fo", 2), ("fo", 3), ("fo", 4), ("mapn", 2),
+    ("mapn", 3), ("mapn", 4), ("fl", 0), ("imgw", 0), ("fn", 0), ("fn", 1), ("fn", 2), ("fn", 3), ("wt", 0),
+    ("mid", 0), ("fn", 4), ("mid", 1), ("flf", 0), ("inv", 0), ("mid", 2), ("inv", 1), ("mid", 3), ("mid", 4),
+    ("mid", 5), ("inv", 2), ("inv", 3), ("inv", 4),
 )
 
 
 def kernel_body(
-    n, image, sens, weight, fy, fzt, fx, hx, hzt, hy, out,
-    sent, got, home, rows, halo, filt, spread, maps, images, mine, sums, parts, totals,
-    send1, recv1, send2, recv2, hsend, hrecv, wsem, msend, mrecv, isend, irecv, tsend, trecv,
+    n, image_in, sens_in, weight, *rest,
 ):
+    names, rest = rest[:6], rest[6:]
+    (out, image, sens, fy, fzt, fx, hx, hzt, hy, load, sent, got, home, rows, halo, filt, spread, maps, images, mine, sums, parts, totals,
+    send1, recv1, send2, recv2, hsend, hrecv, wsem, msend, mrecv, isend, irecv, tsend, trecv) = rest
     me = lax.axis_index("slab")
     coils, _, xs, ny, nz = sens.shape
     gx, gz = fx.shape[0] // 2, weight.shape[1]
@@ -86,6 +87,14 @@
 
     def if_end(body):
         pl.when(jnp.logical_not(is_mid))(body)
+
+    loads = [
+        pltpu.make_async_copy(source, target, load.at[i])
+        for i, (source, target) in enumerate(zip(
+            (sens_in, image_in, *names), (sens, image, fy, fzt, fx, hx, hzt, hy)))
+    ]
+    for copy in loads:
+        copy.start()
 
     columns = [
         pltpu.make_async_copy(weight.at[:, pl.ds(i * 128, 128)], filt.at[i], wsem.at[i])
@@ -408,6 +417,19 @@
             home[last, me] = got[last, me]
 
     def spread_filter(c):
+        @pl.when(me < n - 1)
+        def _():
+            for p in range(2):
+                halo_copy(p, 0).start()
+
+        @pl.when(me > 0)
+        def _():
+            for p in range(2):
+                halo_copy(p, 1).start()
+
+        sums[...] = jnp.zeros_like(sums)
+        out[...] = jnp.zeros_like(out)
+
         for copy in columns:
             copy.wait()
 
@@ -424,20 +446,11 @@
         "fl": forward_last, "flf": forward_last_far, "mid": whole_middle, "inv": inverse,
     }
 
+    for copy in loads:
+        copy.wait()
+
     mine[...] = image[...].astype(BF16)
 
-    @pl.when(me < n - 1)
-    def _():
-        for p in range(2):
-            halo_copy(p, 0).start()
-
-    @pl.when(me > 0)
-    def _():
-        for p in range(2):
-            halo_copy(p, 1).start()
-
-    sums[...] = jnp.zeros_like(sums)
-    out[...] = jnp.zeros_like(out)
     @pl.loop(0, max(len(MID_ORDER), len(END_ORDER)))
     def _(t):
         for name, body in steps.items():
@@ -532,9 +545,13 @@
     return pl.pallas_call(
         functools.partial(kernel_body, n),
         out_shape=jax.ShapeDtypeStruct(image.shape, F32),
-        in_specs=[vmem] * 2 + [pl.BlockSpec(memory_space=pl.ANY)] + [vmem] * 6,
+        in_specs=[pl.BlockSpec(memory_space=pl.ANY)] * 9,
         out_specs=vmem,
         scratch_shapes=[
+            pltpu.VMEM(image.shape, F32),
+            pltpu.VMEM(sensitivity.shape, BF16),
+            *[pltpu.VMEM(t.shape, BF16) for t in tables],
+            dma((8,)),
             pltpu.VMEM((coils, slots, *block), BF16),
             pltpu.VMEM((coils, n, *block), BF16),
             pltpu.VMEM((coils, slots, *block), BF16),

time: 247 us -> 241 us (0.976)
  Pallas kernels: 242 us -> 234 us
    pallas_call x1, Pallas kernels: 242 us -> 234 us  [fused(): pl.pallas_call(functools.partial(kernel_body, n), out_shape=jax.ShapeDtyp...]
where the time goes in v3:
time: 241 us; the launch traced here: 236 us
  Pallas kernels  234 us (97%)
    pallas_call x1, Pallas kernels, fused(): pl.pallas_call(functools.partial(kernel_body, n), out_shape=jax.ShapeDtyp...  234 us

profile of v3, /device:TPU:27, one launch (start us, length us, event | category | flops | bytes accessed | tf_op | source)
XLA Modules:
  0.0 236.4 jit_solution(112439630761729798)
XLA Ops:
  0.0 234.1 %shard_map.91 = f32[2,8,128,128]{3,2,1,0:T(8,128)} custom-call(f32[2,8,128,128]{3,2,1,0:T(8,128)} %image_in.1, bf16[6,2,8,128,128]{4,3,2,1,0:T(8,128)(2,1)} %sens_in.1, f32[4096,256]{1,0:T(8,128)} %bitcast.1, bf16[512,256]{1,0:T(8,128)(2,1)} %constant.8.clone.rest_0_, bf16[256,512]{1,0:T(8,128)(2,1)} %constant.9.clone.rest_1_.rest_3_, ...), custom_call_target="tpu_custom_call" | custom-call | tf_op jit(solution)/shard_map/pallas_call | solution.py:545
  234.1 2.3 copy.11
